TPU v7x, 32 devices: a whole 2x2x4 slice. The times are simulated.
32 devices in a mesh: dp: 8 (over z, x), tensor: 4 (over y, core).
Axes of the slice: x: 2, y: 2, z: 4, core: 2. Of those that a mesh axis runs over, the one named last changes fastest.
Arguments:
- activations: bfloat16 [16, 128, 4096], P('dp'), may hold values from -6 to 6
- out_grads: bfloat16 [16, 128, 20480], P('dp', None, 'tensor'), may hold values from -0.875 to 0.875
- act_scale: bfloat16 [16, 32], P('dp'), may hold values from 1 to 16
- grad_scale: bfloat16 [16, 1, 20480], P('dp', None, 'tensor'), may hold values from 1 to 72
- moment: float32 [20480, 4096], P(('tensor', 'dp')), may hold values from -0.6 to 0.6
- second: float32 [20480, 4096], P(('tensor', 'dp')), may hold values from 0.1 to 1
- master: float32 [20480, 4096], P(('tensor', 'dp')), may hold values from -0.0625 to 0.0625
Outputs:
- new_moment: float32 [20480, 4096], P(('tensor', 'dp'))
- new_second: float32 [20480, 4096], P(('tensor', 'dp'))
- new_master: float32 [20480, 4096], P(('tensor', 'dp'))
- weights: bfloat16 [20480, 4096], P(('tensor', 'dp'))
All inputs are finite; a program needn't handle non-finite values.
Results may differ from a plain program's by a relative error of at most 0.015.
Values may be sent and summed in bfloat16 or wider, within the bound.
A program may use at most 192 MiB of HBM per device.

v0:
```python
import jax
import jax.numpy as jnp
from jax import lax
from jax.sharding import PartitionSpec as P

FF = 20480
ROWS = 4096
TILE = 128
clip_rms = 1.0
beta_first = 0.9
beta_second = 0.95
learn_rate = 0.003
adam_eps = 1e-08


def widen(act_scale):
    tiles = act_scale.astype(jnp.float32)
    spread = jnp.broadcast_to(tiles[:, :, None], tiles.shape + (TILE,))
    return spread.reshape(tiles.shape[0], tiles.shape[1] * TILE)


def transposed_product(grads_rows, acts_rows):
    return lax.dot_general(
        grads_rows, acts_rows, (((0,), (0,)), ((), ())), preferred_element_type=jnp.float32
    )


def per_device(activations, out_grads, act_scale, grad_scale, moment, second, master):
    owners = lax.axis_size("dp")
    owned = out_grads.shape[2] // owners
    weight_rows = activations.shape[2]
    local_tokens = activations.shape[0] * activations.shape[1]
    acts_deq = (
        (activations.astype(jnp.float32) * widen(act_scale)[:, None, :])
        .astype(jnp.bfloat16)
        .reshape(local_tokens, weight_rows)
    )
    grads_deq = (
        (out_grads.astype(jnp.float32) * grad_scale.astype(jnp.float32))
        .astype(jnp.bfloat16)
        .reshape(local_tokens, out_grads.shape[2])
    )
    moved = lax.all_to_all(grads_deq, "dp", split_axis=1, concat_axis=0, tiled=True)
    piece = lax.all_gather(acts_deq, "dp", axis=0, tiled=True)
    count = piece.shape[0]

    def add_group(group, total):
        offset = (group * local_tokens).astype(jnp.int32)
        acts_group = lax.dynamic_slice_in_dim(piece, offset, local_tokens, 0)
        grads_group = lax.dynamic_slice_in_dim(moved, offset, local_tokens, 0)
        term = transposed_product(grads_group, acts_group)
        rounded = lax.optimization_barrier(term.astype(jnp.bfloat16))
        return total + rounded.astype(jnp.float32)

    grad_owned = lax.fori_loop(
        0, count // local_tokens, add_group, jnp.zeros((owned, weight_rows), jnp.float32)
    )
    squares = lax.psum(jnp.sum(grad_owned * grad_owned), ("dp", "tensor"))
    limit = clip_rms * jnp.sqrt(jnp.float32(FF * ROWS))
    factor = jnp.minimum(1.0, limit / jnp.sqrt(squares))
    clipped = factor * grad_owned
    new_moment = beta_first * moment + (1.0 - beta_first) * clipped
    new_second = beta_second * second + (1.0 - beta_second) * clipped * clipped
    new_master = master - learn_rate * new_moment / (jnp.sqrt(new_second) + adam_eps)
    weights = new_master.astype(jnp.bfloat16)
    return (new_moment, new_second, new_master, weights)


def solution(mesh):
    return jax.shard_map(
        per_device,
        mesh=mesh,
        in_specs=(
            P("dp", None, None),
            P("dp", None, "tensor"),
            P("dp", None),
            P("dp", None, "tensor"),
            P(("tensor", "dp"), None),
            P(("tensor", "dp"), None),
            P(("tensor", "dp"), None),
        ),
        out_specs=(
            P(("tensor", "dp"), None),
            P(("tensor", "dp"), None),
            P(("tensor", "dp"), None),
            P(("tensor", "dp"), None),
        ),
        check_vma=False,
    )
```

profile of v0, /device:TPU:0, one launch (start us, length us, event | category | flops | bytes accessed | tf_op | source)
XLA Modules:
  0.0 516.6 jit_solution(14019932499861952802)
XLA Ops:
  7.2 0.0 all-gather.2.cloned.1.call-start
  7.2 0.7 convert_element_type.36
  7.9 0.1 broadcast_bitcast_fusion
  8.0 3.4 multiply_convert_fusion.1
  11.4 0.0 all-gather.2.cloned.1.call-update
  11.4 0.7 bitcast_convert_fusion
  12.1 2.3 multiply_convert_fusion
  14.5 0.5 copy.12
  15.0 1.8 copy.11
  16.8 7.3 %all-to-all-start = ((bf16[256,8,640]{2,0,1:T(8,128)(2,1)}), bf16[256,8,640]{2,0,1:T(8,128)(2,1)S(1)}, u32[]{:S(2)}, u32[]{:S(2)}) async-start(bf16[256,8,640]{2,0,1:T(8,128)(2,1)} %copy.11), calls=%async_computation | async-start | bytes 5242880 | tf_op jit(solution)/shard_map/all_to_all | solution.py:43
  24.1 121.2 %all-to-all-done = bf16[256,8,640]{2,0,1:T(8,128)(2,1)S(1)} async-done(((bf16[256,8,640]{2,0,1:T(8,128)(2,1)}), bf16[256,8,640]{2,0,1:T(8,128)(2,1)S(1)}, u32[]{:S(2)}, u32[]{:S(2)}) %all-to-all-start) | async-done | bytes 2621472 | tf_op jit(solution)/shard_map/all_to_all | solution.py:43
  145.3 151.2 %all-gather.2.cloned.1.call-done = bf16[2048,4096]{1,0:T(8,128)(2,1)} async-done(((bf16[256,4096]{1,0:T(8,128)(2,1)}), bf16[2048,4096]{1,0:T(8,128)(2,1)}) %all-gather.2.cloned.1.call-update) | async-done | bytes 16777232 | tf_op jit(solution)/shard_map/all_gather | solution.py:44
  296.5 137.7 %while.14 = (s32[]{:T(128)}, f32[640,4096]{1,0:T(8,128)}, bf16[2048,640]{1,0:T(8,128)(2,1)S(1)}, bf16[2048,4096]{1,0:T(8,128)(2,1)}, s32[]{:T(128)}, /*index=5*/s32[]{:T(128)}, s32[]{:T(128)}, s32[]{:T(128)}) while((s32[]{:T(128)}, f32[640,4096]{1,0:T(8,128)}, bf16[2048,640]{1,0:T(8,128)(2,1)S(1)}, bf16[2048,4096]{1,0:T(8,128)(2,1)}, ...), condition=%wide.region_1.0_spmd.clone, body=%wide.region_0.0_spmd.clone.sunk | while | flops 1352663040 | bytes 33883284 | solution.py:55
  296.5 5.5 %convolution_convert_fusion.2 = bf16[640,4096]{1,0:T(8,128)(2,1)} fusion(bf16[2048,4096]{1,0:T(8,128)(2,1)} %get-tuple-element.155, s32[]{:T(128)S(6)} %select_n.10, bf16[2048,640]{1,0:T(8,128)(2,1)S(1)} %get-tuple-element.154), kind=kOutput, calls=%fused_computation.1.clone.1 | convolution fusion | flops 1344798720 | bytes 7668736 | tf_op jit(solution)/shard_map/while/body/eval_jaxpr/dot_general | solution.py:23
  302.0 9.1 %select_add_fusion.2 = f32[640,4096]{1,0:T(8,128)} fusion(f32[640,4096]{1,0:T(8,128)} %get-tuple-element.145, bf16[640,4096]{1,0:T(8,128)(2,1)} %convolution_convert_fusion.2, pred[]{:T(512)S(6)} %compare.3), kind=kLoop, calls=%fused_computation.clone.1 | loop fusion | flops 7864320 | bytes 26214400 | tf_op jit(solution)/shard_map/while/body/eval_jaxpr/add | solution.py:53
  311.1 5.5 %convolution_convert_fusion.2 = bf16[640,4096]{1,0:T(8,128)(2,1)} fusion(bf16[2048,4096]{1,0:T(8,128)(2,1)} %get-tuple-element.155, s32[]{:T(128)S(6)} %select_n.10, bf16[2048,640]{1,0:T(8,128)(2,1)S(1)} %get-tuple-element.154), kind=kOutput, calls=%fused_computation.1.clone.1 | convolution fusion | flops 1344798720 | bytes 7668736 | tf_op jit(solution)/shard_map/while/body/eval_jaxpr/dot_general | solution.py:23
  316.6 12.1 %select_add_fusion.2 = f32[640,4096]{1,0:T(8,128)} fusion(f32[640,4096]{1,0:T(8,128)} %get-tuple-element.145, bf16[640,4096]{1,0:T(8,128)(2,1)} %convolution_convert_fusion.2, pred[]{:T(512)S(6)} %compare.3), kind=kLoop, calls=%fused_computation.clone.1 | loop fusion | flops 7864320 | bytes 26214400 | tf_op jit(solution)/shard_map/while/body/eval_jaxpr/add | solution.py:53
  328.7 5.5 %convolution_convert_fusion.2 = bf16[640,4096]{1,0:T(8,128)(2,1)} fusion(bf16[2048,4096]{1,0:T(8,128)(2,1)} %get-tuple-element.155, s32[]{:T(128)S(6)} %select_n.10, bf16[2048,640]{1,0:T(8,128)(2,1)S(1)} %get-tuple-element.154), kind=kOutput, calls=%fused_computation.1.clone.1 | convolution fusion | flops 1344798720 | bytes 7668736 | tf_op jit(solution)/shard_map/while/body/eval_jaxpr/dot_general | solution.py:23
  334.2 12.1 %select_add_fusion.2 = f32[640,4096]{1,0:T(8,128)} fusion(f32[640,4096]{1,0:T(8,128)} %get-tuple-element.145, bf16[640,4096]{1,0:T(8,128)(2,1)} %convolution_convert_fusion.2, pred[]{:T(512)S(6)} %compare.3), kind=kLoop, calls=%fused_computation.clone.1 | loop fusion | flops 7864320 | bytes 26214400 | tf_op jit(solution)/shard_map/while/body/eval_jaxpr/add | solution.py:53
  346.3 5.5 %convolution_convert_fusion.2 = bf16[640,4096]{1,0:T(8,128)(2,1)} fusion(bf16[2048,4096]{1,0:T(8,128)(2,1)} %get-tuple-element.155, s32[]{:T(128)S(6)} %select_n.10, bf16[2048,640]{1,0:T(8,128)(2,1)S(1)} %get-tuple-element.154), kind=kOutput, calls=%fused_computation.1.clone.1 | convolution fusion | flops 1344798720 | bytes 7668736 | tf_op jit(solution)/shard_map/while/body/eval_jaxpr/dot_general | solution.py:23
  351.8 12.1 %select_add_fusion.2 = f32[640,4096]{1,0:T(8,128)} fusion(f32[640,4096]{1,0:T(8,128)} %get-tuple-element.145, bf16[640,4096]{1,0:T(8,128)(2,1)} %convolution_convert_fusion.2, pred[]{:T(512)S(6)} %compare.3), kind=kLoop, calls=%fused_computation.clone.1 | loop fusion | flops 7864320 | bytes 26214400 | tf_op jit(solution)/shard_map/while/body/eval_jaxpr/add | solution.py:53
  363.9 5.5 %convolution_convert_fusion.2 = bf16[640,4096]{1,0:T(8,128)(2,1)} fusion(bf16[2048,4096]{1,0:T(8,128)(2,1)} %get-tuple-element.155, s32[]{:T(128)S(6)} %select_n.10, bf16[2048,640]{1,0:T(8,128)(2,1)S(1)} %get-tuple-element.154), kind=kOutput, calls=%fused_computation.1.clone.1 | convolution fusion | flops 1344798720 | bytes 7668736 | tf_op jit(solution)/shard_map/while/body/eval_jaxpr/dot_general | solution.py:23
  369.4 12.1 %select_add_fusion.2 = f32[640,4096]{1,0:T(8,128)} fusion(f32[640,4096]{1,0:T(8,128)} %get-tuple-element.145, bf16[640,4096]{1,0:T(8,128)(2,1)} %convolution_convert_fusion.2, pred[]{:T(512)S(6)} %compare.3), kind=kLoop, calls=%fused_computation.clone.1 | loop fusion | flops 7864320 | bytes 26214400 | tf_op jit(solution)/shard_map/while/body/eval_jaxpr/add | solution.py:53
  381.5 5.5 %convolution_convert_fusion.2 = bf16[640,4096]{1,0:T(8,128)(2,1)} fusion(bf16[2048,4096]{1,0:T(8,128)(2,1)} %get-tuple-element.155, s32[]{:T(128)S(6)} %select_n.10, bf16[2048,640]{1,0:T(8,128)(2,1)S(1)} %get-tuple-element.154), kind=kOutput, calls=%fused_computation.1.clone.1 | convolution fusion | flops 1344798720 | bytes 7668736 | tf_op jit(solution)/shard_map/while/body/eval_jaxpr/dot_general | solution.py:23
  387.0 12.1 %select_add_fusion.2 = f32[640,4096]{1,0:T(8,128)} fusion(f32[640,4096]{1,0:T(8,128)} %get-tuple-element.145, bf16[640,4096]{1,0:T(8,128)(2,1)} %convolution_convert_fusion.2, pred[]{:T(512)S(6)} %compare.3), kind=kLoop, calls=%fused_computation.clone.1 | loop fusion | flops 7864320 | bytes 26214400 | tf_op jit(solution)/shard_map/while/body/eval_jaxpr/add | solution.py:53
  399.1 5.5 %convolution_convert_fusion.2 = bf16[640,4096]{1,0:T(8,128)(2,1)} fusion(bf16[2048,4096]{1,0:T(8,128)(2,1)} %get-tuple-element.155, s32[]{:T(128)S(6)} %select_n.10, bf16[2048,640]{1,0:T(8,128)(2,1)S(1)} %get-tuple-element.154), kind=kOutput, calls=%fused_computation.1.clone.1 | convolution fusion | flops 1344798720 | bytes 7668736 | tf_op jit(solution)/shard_map/while/body/eval_jaxpr/dot_general | solution.py:23
  404.6 12.1 %select_add_fusion.2 = f32[640,4096]{1,0:T(8,128)} fusion(f32[640,4096]{1,0:T(8,128)} %get-tuple-element.145, bf16[640,4096]{1,0:T(8,128)(2,1)} %convolution_convert_fusion.2, pred[]{:T(512)S(6)} %compare.3), kind=kLoop, calls=%fused_computation.clone.1 | loop fusion | flops 7864320 | bytes 26214400 | tf_op jit(solution)/shard_map/while/body/eval_jaxpr/add | solution.py:53
  416.7 5.5 %convolution_convert_fusion.2 = bf16[640,4096]{1,0:T(8,128)(2,1)} fusion(bf16[2048,4096]{1,0:T(8,128)(2,1)} %get-tuple-element.155, s32[]{:T(128)S(6)} %select_n.10, bf16[2048,640]{1,0:T(8,128)(2,1)S(1)} %get-tuple-element.154), kind=kOutput, calls=%fused_computation.1.clone.1 | convolution fusion | flops 1344798720 | bytes 7668736 | tf_op jit(solution)/shard_map/while/body/eval_jaxpr/dot_general | solution.py:23
  422.2 12.1 %select_add_fusion.2 = f32[640,4096]{1,0:T(8,128)} fusion(f32[640,4096]{1,0:T(8,128)} %get-tuple-element.145, bf16[640,4096]{1,0:T(8,128)(2,1)} %convolution_convert_fusion.2, pred[]{:T(512)S(6)} %compare.3), kind=kLoop, calls=%fused_computation.clone.1 | loop fusion | flops 7864320 | bytes 26214400 | tf_op jit(solution)/shard_map/while/body/eval_jaxpr/add | solution.py:53
  434.2 7.3 %multiply_reduce_fusion = f32[]{:T(128)} fusion(f32[640,4096]{1,0:T(8,128)} %get-tuple-element.83), kind=kLoop, calls=%fused_computation.9 | loop fusion | flops 5242879 | bytes 10485764 | tf_op jit(solution)/shard_map/reduce_sum | solution.py:58
  441.5 38.6 %psum.7 = f32[]{:T(128)} all-reduce(f32[]{:T(128)} %multiply_reduce_fusion), channel_id=1, replica_groups=mesh['dp'=8,'tensor'=4] {'dp','tensor'}, use_global_device_ids=true, to_apply=%region_3.0 | all-reduce | flops 1 | bytes 8 | tf_op jit(solution)/shard_map/psum | solution.py:58
  480.8 28.9 %fusion.4 = (bf16[640,4096]{1,0:T(8,128)(2,1)}, f32[640,4096]{1,0:T(8,128)}, f32[640,4096]{1,0:T(8,128)}, f32[640,4096]{1,0:T(8,128)}) fusion(f32[640,4096]{1,0:T(8,128)} %param.15, f32[640,4096]{1,0:T(8,128)} %get-tuple-element.83, f32[]{:T(128)S(6)} %min.3, f32[640,4096]{1,0:T(8,128)} %param.14, f32[640,4096]{1,0:T(8,128)} %param.13), kind=kLoop, calls=%fused_computation.15 | loop fusion | flops 34078720 | bytes 78643200 | tf_op jit(solution)/shard_map/convert_element_type | solution.py:65
  (2 shorter events, 0.0 us)
Async XLA Ops:
  7.2 289.4 %all-gather.2.cloned.1.call-start = ((), (), s32[]{:S(2)}) async-start(), calls=%async_computation.1 | async-start | bytes 18874368 | tf_op jit(solution)/shard_map/all_gather | solution.py:44
  16.8 128.5 %all-to-all-start = ((bf16[256,8,640]{2,0,1:T(8,128)(2,1)}), bf16[256,8,640]{2,0,1:T(8,128)(2,1)S(1)}, u32[]{:S(2)}, u32[]{:S(2)}) async-start(bf16[256,8,640]{2,0,1:T(8,128)(2,1)} %copy.11), calls=%async_computation | async-start | bytes 5242880 | tf_op jit(solution)/shard_map/all_to_all | solution.py:43
Sparse Core Ops, SparseCore 0:
  11.5 284.9 all-gather.1
where the time goes:
time: 517 us
  waiting for transfers between devices  272 us (53%)
  other arithmetic  137 us (26%)
  matrix products  44 us (9%)
  blocking collectives  38.6 us (7%)
  between operations  14.8 us (3%)
  starting transfers between devices  7.32 us (1%)
    all_gather x1, waiting for transfers between devices, per_device(): piece = lax.all_gather(acts_deq, 'dp', axis=0, tiled=True)  151 us
    all_to_all x1, waiting for transfers between devices, per_device(): lax.all_to_all(grads_deq, 'dp', split_axis=1, concat_axis=0, tiled=True)  121 us
    add x8, other arithmetic, add_group(): return total + rounded.astype(jnp.float32)  93.7 us
    dot_general x8, matrix products, transposed_product(): lax.dot_general(grads_rows, acts_rows, (((0,), (0,)), ((), ())), preferre...  44 us
    psum x1, blocking collectives, per_device(): squares = lax.psum(jnp.sum(grad_owned * grad_owned), ('dp', 'tensor'))  38.6 us
    convert_element_type x1, other arithmetic, per_device(): weights = new_master.astype(jnp.bfloat16)  28.9 us
  transfers between devices with their start and end apart: 2, of which 2 were waited for; matrix products, arithmetic and copies ran while one was open for 1% of the time, Pallas kernels for 0%

commit v1 on v0

--- a/solution.py
+++ b/solution.py
@@ -41,7 +41,12 @@
         .reshape(local_tokens, out_grads.shape[2])
     )
     moved = lax.all_to_all(grads_deq, "dp", split_axis=1, concat_axis=0, tiled=True)
-    piece = lax.all_gather(acts_deq, "dp", axis=0, tiled=True)
+    ring = [acts_deq]
+    for hop in range(7):
+        ring.append(lax.ppermute(ring[-1], "dp", [(dev, (dev + 1) % 8) for dev in range(8)]))
+    piece = jnp.roll(
+        jnp.concatenate(ring[::-1], axis=0), (lax.axis_index("dp") + 1) * ring[0].shape[0], axis=0
+    )
     count = piece.shape[0]
 
     def add_group(group, total):

time: 517 us -> 616 us (1.19)
  waiting for transfers between devices: 272 us -> 341 us
  local copies, waits for them, and re-layouts: 2.41 us -> 28.1 us
  blocking collectives: 38.6 us -> 53.5 us
  between operations: 14.8 us -> 1.56 us
    ppermute x0 -> x7, waiting for transfers between devices: none -> 341 us  [per_device(): lax.ppermute(ring[-1], 'dp', [(dev, (dev + 1) % 8) for dev in range(8)])]
    all_gather x1 -> x0, waiting for transfers between devices: 151 us -> none  [per_device(): piece = lax.all_gather(acts_deq, 'dp', axis=0, tiled=True)]
    all_to_all x1, waiting for transfers between devices: 121 us -> 0.01 us  [per_device(): lax.all_to_all(grads_deq, 'dp', split_axis=1, concat_axis=0, tiled=True)]
    unnamed x3 -> x36, local copies, waits for them, and re-layouts: 0.59 us -> 19.6 us
    psum x1, blocking collectives: 38.6 us -> 53.5 us  [per_device(): squares = lax.psum(jnp.sum(grad_owned * grad_owned), ('dp', 'tensor'))]
    dynamic_slice x0 -> x1, local copies, waits for them, and re-layouts: none -> 6.55 us  [per_device(): jnp.roll(jnp.concatenate(ring[::-1], axis=0), (lax.axis_index('dp') + 1)...]
  transfers between devices with their start and end apart: 2 -> 8, of which waited for: 2 -> 7; matrix products, arithmetic and copies ran while one was open for 1% -> 4% of each run, Pallas kernels for 0% -> 0%
where the time goes in v1:
time: 616 us; the launch traced here: 614 us
  waiting for transfers between devices  341 us (55%)
  other arithmetic  136 us (22%)
  blocking collectives  53.5 us (9%)
  matrix products  45 us (7%)
  local copies, waits for them, and re-layouts  28.1 us (5%)
  starting transfers between devices  9.03 us (1%)
    ppermute x7, waiting for transfers between devices, per_device(): lax.ppermute(ring[-1], 'dp', [(dev, (dev + 1) % 8) for dev in range(8)])  341 us
    add x8, other arithmetic, add_group(): return total + rounded.astype(jnp.float32)  93.7 us
    psum x1, blocking collectives, per_device(): squares = lax.psum(jnp.sum(grad_owned * grad_owned), ('dp', 'tensor'))  53.5 us
    dot_general x8, matrix products, transposed_product(): lax.dot_general(grads_rows, acts_rows, (((0,), (0,)), ((), ())), preferre...  45 us
    convert_element_type x1, other arithmetic, per_device(): weights = new_master.astype(jnp.bfloat16)  28.9 us
    unnamed x36, local copies, waits for them, and re-layouts  19.6 us
  transfers between devices with their start and end apart: 8, of which 7 were waited for; matrix products, arithmetic and copies ran while one was open for 4% of the time, Pallas kernels for 0%

profile of v1, /device:TPU:0, one launch (start us, length us, event | category | flops | bytes accessed | tf_op | source)
XLA Modules:
  0.0 614.3 jit_solution(12160294107542235938)
XLA Ops:
  1.4 2.1 multiply_convert_fusion.1
  3.5 3.0 collective-permute-start
  6.5 48.7 %collective-permute-done = bf16[256,4096]{1,0:T(8,128)(2,1)S(1)} collective-permute-done((bf16[256,4096]{1,0:T(8,128)(2,1)S(1)}, bf16[256,4096]{1,0:T(8,128)(2,1)S(1)}, u32[]{:S(2)}, u32[]{:S(2)}) %collective-permute-start) | collective-permute-done | bytes 2097184 | tf_op jit(solution)/shard_map/ppermute | solution.py:46
  56.5 49.5 %collective-permute-done.1 = bf16[256,4096]{1,0:T(8,128)(2,1)S(1)} collective-permute-done((bf16[256,4096]{1,0:T(8,128)(2,1)S(1)}, bf16[256,4096]{1,0:T(8,128)(2,1)S(1)}, u32[]{:S(2)}, u32[]{:S(2)}) %collective-permute-start.1) | collective-permute-done | bytes 2097184 | tf_op jit(solution)/shard_map/ppermute | solution.py:46
  107.3 48.6 %collective-permute-done.2 = bf16[256,4096]{1,0:T(8,128)(2,1)S(1)} collective-permute-done((bf16[256,4096]{1,0:T(8,128)(2,1)S(1)}, bf16[256,4096]{1,0:T(8,128)(2,1)S(1)}, u32[]{:S(2)}, u32[]{:S(2)}) %collective-permute-start.2) | collective-permute-done | bytes 2097184 | tf_op jit(solution)/shard_map/ppermute | solution.py:46
  157.3 47.8 %collective-permute-done.3 = bf16[256,4096]{1,0:T(8,128)(2,1)S(1)} collective-permute-done((bf16[256,4096]{1,0:T(8,128)(2,1)S(1)}, bf16[256,4096]{1,0:T(8,128)(2,1)S(1)}, u32[]{:S(2)}, u32[]{:S(2)}) %collective-permute-start.3) | collective-permute-done | bytes 2097184 | tf_op jit(solution)/shard_map/ppermute | solution.py:46
  206.4 46.9 %collective-permute-done.4 = bf16[256,4096]{1,0:T(8,128)(2,1)S(1)} collective-permute-done((bf16[256,4096]{1,0:T(8,128)(2,1)S(1)}, bf16[256,4096]{1,0:T(8,128)(2,1)S(1)}, u32[]{:S(2)}, u32[]{:S(2)}) %collective-permute-start.4) | collective-permute-done | bytes 2097184 | tf_op jit(solution)/shard_map/ppermute | solution.py:46
  254.7 46.2 %collective-permute-done.5 = bf16[256,4096]{1,0:T(8,128)(2,1)} collective-permute-done((bf16[256,4096]{1,0:T(8,128)(2,1)S(1)}, bf16[256,4096]{1,0:T(8,128)(2,1)}, u32[]{:S(2)}, u32[]{:S(2)}) %collective-permute-start.5) | collective-permute-done | bytes 2097184 | tf_op jit(solution)/shard_map/ppermute | solution.py:46
  301.6 2.3 multiply_convert_fusion
  306.2 6.0 all-to-all-start
  312.3 53.8 %collective-permute-done.6 = bf16[256,4096]{1,0:T(8,128)(2,1)} collective-permute-done((bf16[256,4096]{1,0:T(8,128)(2,1)}, bf16[256,4096]{1,0:T(8,128)(2,1)}, u32[]{:S(2)}, u32[]{:S(2)}) %collective-permute-start.6) | collective-permute-done | bytes 2097184 | tf_op jit(solution)/shard_map/ppermute | solution.py:46
  378.7 6.5 %constant_dynamic-slice_fusion = bf16[2048,4096]{1,0:T(8,128)(2,1)} fusion(bf16[4096,4096]{1,0:T(8,128)(2,1)S(1)} %constant_dynamic-update-slice_fusion, s32[]{:T(128)S(6)} %select_n.22), kind=kLoop, calls=%fused_computation.31 | loop fusion | bytes 33554436 | tf_op jit(solution)/shard_map/jit(_roll_dynamic)/dynamic_slice | solution.py:47
  385.3 138.7 %while.14 = (s32[]{:T(128)}, f32[640,4096]{1,0:T(8,128)}, bf16[2048,640]{1,0:T(8,128)(2,1)}, bf16[2048,4096]{1,0:T(8,128)(2,1)}, s32[]{:T(128)}, /*index=5*/s32[]{:T(128)}, s32[]{:T(128)}, s32[]{:T(128)}) while((s32[]{:T(128)}, f32[640,4096]{1,0:T(8,128)}, bf16[2048,640]{1,0:T(8,128)(2,1)}, bf16[2048,4096]{1,0:T(8,128)(2,1)}, ...), condition=%wide.region_1.2_spmd.clone, body=%wide.region_0.1_spmd.clone.sunk | while | flops 1352663040 | bytes 33883276 | solution.py:60
  385.3 5.6 convolution_convert_fusion.2
  390.9 9.1 %select_add_fusion.2 = f32[640,4096]{1,0:T(8,128)} fusion(f32[640,4096]{1,0:T(8,128)} %get-tuple-element.145, bf16[640,4096]{1,0:T(8,128)(2,1)} %convolution_convert_fusion.2, pred[]{:T(512)S(6)} %compare.4), kind=kLoop, calls=%fused_computation.clone.1 | loop fusion | flops 7864320 | bytes 26214400 | tf_op jit(solution)/shard_map/while/body/eval_jaxpr/add | solution.py:58
  400.0 5.6 convolution_convert_fusion.2
  405.6 12.1 %select_add_fusion.2 = f32[640,4096]{1,0:T(8,128)} fusion(f32[640,4096]{1,0:T(8,128)} %get-tuple-element.145, bf16[640,4096]{1,0:T(8,128)(2,1)} %convolution_convert_fusion.2, pred[]{:T(512)S(6)} %compare.4), kind=kLoop, calls=%fused_computation.clone.1 | loop fusion | flops 7864320 | bytes 26214400 | tf_op jit(solution)/shard_map/while/body/eval_jaxpr/add | solution.py:58
  417.7 5.6 convolution_convert_fusion.2
  423.3 12.1 %select_add_fusion.2 = f32[640,4096]{1,0:T(8,128)} fusion(f32[640,4096]{1,0:T(8,128)} %get-tuple-element.145, bf16[640,4096]{1,0:T(8,128)(2,1)} %convolution_convert_fusion.2, pred[]{:T(512)S(6)} %compare.4), kind=kLoop, calls=%fused_computation.clone.1 | loop fusion | flops 7864320 | bytes 26214400 | tf_op jit(solution)/shard_map/while/body/eval_jaxpr/add | solution.py:58
  435.4 5.6 convolution_convert_fusion.2
  441.0 12.1 %select_add_fusion.2 = f32[640,4096]{1,0:T(8,128)} fusion(f32[640,4096]{1,0:T(8,128)} %get-tuple-element.145, bf16[640,4096]{1,0:T(8,128)(2,1)} %convolution_convert_fusion.2, pred[]{:T(512)S(6)} %compare.4), kind=kLoop, calls=%fused_computation.clone.1 | loop fusion | flops 7864320 | bytes 26214400 | tf_op jit(solution)/shard_map/while/body/eval_jaxpr/add | solution.py:58
  453.1 5.6 convolution_convert_fusion.2
  458.7 12.1 %select_add_fusion.2 = f32[640,4096]{1,0:T(8,128)} fusion(f32[640,4096]{1,0:T(8,128)} %get-tuple-element.145, bf16[640,4096]{1,0:T(8,128)(2,1)} %convolution_convert_fusion.2, pred[]{:T(512)S(6)} %compare.4), kind=kLoop, calls=%fused_computation.clone.1 | loop fusion | flops 7864320 | bytes 26214400 | tf_op jit(solution)/shard_map/while/body/eval_jaxpr/add | solution.py:58
  470.8 5.6 convolution_convert_fusion.2
  476.4 12.1 %select_add_fusion.2 = f32[640,4096]{1,0:T(8,128)} fusion(f32[640,4096]{1,0:T(8,128)} %get-tuple-element.145, bf16[640,4096]{1,0:T(8,128)(2,1)} %convolution_convert_fusion.2, pred[]{:T(512)S(6)} %compare.4), kind=kLoop, calls=%fused_computation.clone.1 | loop fusion | flops 7864320 | bytes 26214400 | tf_op jit(solution)/shard_map/while/body/eval_jaxpr/add | solution.py:58
  488.5 5.6 convolution_convert_fusion.2
  494.1 12.1 %select_add_fusion.2 = f32[640,4096]{1,0:T(8,128)} fusion(f32[640,4096]{1,0:T(8,128)} %get-tuple-element.145, bf16[640,4096]{1,0:T(8,128)(2,1)} %convolution_convert_fusion.2, pred[]{:T(512)S(6)} %compare.4), kind=kLoop, calls=%fused_computation.clone.1 | loop fusion | flops 7864320 | bytes 26214400 | tf_op jit(solution)/shard_map/while/body/eval_jaxpr/add | solution.py:58
  506.2 5.6 convolution_convert_fusion.2
  511.8 12.1 %select_add_fusion.2 = f32[640,4096]{1,0:T(8,128)} fusion(f32[640,4096]{1,0:T(8,128)} %get-tuple-element.145, bf16[640,4096]{1,0:T(8,128)(2,1)} %convolution_convert_fusion.2, pred[]{:T(512)S(6)} %compare.4), kind=kLoop, calls=%fused_computation.clone.1 | loop fusion | flops 7864320 | bytes 26214400 | tf_op jit(solution)/shard_map/while/body/eval_jaxpr/add | solution.py:58
  523.9 7.3 %multiply_reduce_fusion = f32[]{:T(128)} fusion(f32[640,4096]{1,0:T(8,128)} %get-tuple-element.83), kind=kLoop, calls=%fused_computation.9 | loop fusion | flops 5242879 | bytes 10485764 | tf_op jit(solution)/shard_map/reduce_sum | solution.py:63
  531.2 53.5 %psum.7 = f32[]{:T(128)} all-reduce(f32[]{:T(128)} %multiply_reduce_fusion), channel_id=1, replica_groups=mesh['dp'=8,'tensor'=4] {'dp','tensor'}, use_global_device_ids=true, to_apply=%region_3.4 | all-reduce | flops 1 | bytes 8 | tf_op jit(solution)/shard_map/psum | solution.py:63
  585.4 28.9 %fusion.4 = (bf16[640,4096]{1,0:T(8,128)(2,1)}, f32[640,4096]{1,0:T(8,128)}, f32[640,4096]{1,0:T(8,128)}, f32[640,4096]{1,0:T(8,128)}) fusion(f32[640,4096]{1,0:T(8,128)} %param.15, f32[640,4096]{1,0:T(8,128)} %get-tuple-element.83, f32[]{:T(128)S(6)} %min.3, f32[640,4096]{1,0:T(8,128)} %param.14, f32[640,4096]{1,0:T(8,128)} %param.13), kind=kLoop, calls=%fused_computation.32 | loop fusion | flops 34078720 | bytes 78643200 | tf_op jit(solution)/shard_map/convert_element_type | solution.py:70
  (48 shorter events, 23.0 us)
Async XLA Ops:
  3.5 51.7 %collective-permute-start = (bf16[256,4096]{1,0:T(8,128)(2,1)S(1)}, bf16[256,4096]{1,0:T(8,128)(2,1)S(1)}, u32[]{:S(2)}, u32[]{:S(2)}) collective-permute-start(bf16[256,4096]{1,0:T(8,128)(2,1)S(1)} %bitcast.15), channel_id=1, source_target_pairs={{0,4},{4,8},{8,12},{12,16},{16,20},{20,24},{24,28},{28,0},{1,5},{5... | collective-permute-start | bytes 6291464 | tf_op jit(solution)/shard_map/ppermute | solution.py:46
  55.1 1.3 copy-start
  56.5 49.5 %collective-permute-start.1 = (bf16[256,4096]{1,0:T(8,128)(2,1)S(1)}, bf16[256,4096]{1,0:T(8,128)(2,1)S(1)}, u32[]{:S(2)}, u32[]{:S(2)}) collective-permute-start(bf16[256,4096]{1,0:T(8,128)(2,1)S(1)} %collective-permute-done), channel_id=1, source_target_pairs={{0,4},{4,8},{8,12},{12,16},{16,20},{20,24},{24,28},{28,0},{1,5},{5... | collective-permute-start | bytes 6291464 | tf_op jit(solution)/shard_map/ppermute | solution.py:46
  106.0 1.3 copy-start.2
  107.3 48.6 %collective-permute-start.2 = (bf16[256,4096]{1,0:T(8,128)(2,1)S(1)}, bf16[256,4096]{1,0:T(8,128)(2,1)S(1)}, u32[]{:S(2)}, u32[]{:S(2)}) collective-permute-start(bf16[256,4096]{1,0:T(8,128)(2,1)S(1)} %collective-permute-done.1), channel_id=1, source_target_pairs={{0,4},{4,8},{8,12},{12,16},{16,20},{20,24},{24,28},{28,0},{1,5},{5... | collective-permute-start | bytes 6291464 | tf_op jit(solution)/shard_map/ppermute | solution.py:46
  156.0 1.4 copy-start.4
  157.3 47.8 %collective-permute-start.3 = (bf16[256,4096]{1,0:T(8,128)(2,1)S(1)}, bf16[256,4096]{1,0:T(8,128)(2,1)S(1)}, u32[]{:S(2)}, u32[]{:S(2)}) collective-permute-start(bf16[256,4096]{1,0:T(8,128)(2,1)S(1)} %collective-permute-done.2), channel_id=1, source_target_pairs={{0,4},{4,8},{8,12},{12,16},{16,20},{20,24},{24,28},{28,0},{1,5},{5... | collective-permute-start | bytes 6291464 | tf_op jit(solution)/shard_map/ppermute | solution.py:46
  205.1 1.3 copy-start.6
  206.4 46.9 %collective-permute-start.4 = (bf16[256,4096]{1,0:T(8,128)(2,1)S(1)}, bf16[256,4096]{1,0:T(8,128)(2,1)S(1)}, u32[]{:S(2)}, u32[]{:S(2)}) collective-permute-start(bf16[256,4096]{1,0:T(8,128)(2,1)S(1)} %collective-permute-done.3), channel_id=1, source_target_pairs={{0,4},{4,8},{8,12},{12,16},{16,20},{20,24},{24,28},{28,0},{1,5},{5... | collective-permute-start | bytes 6291464 | tf_op jit(solution)/shard_map/ppermute | solution.py:46
  253.4 1.3 copy-start.8
  254.7 46.2 %collective-permute-start.5 = (bf16[256,4096]{1,0:T(8,128)(2,1)S(1)}, bf16[256,4096]{1,0:T(8,128)(2,1)}, u32[]{:S(2)}, u32[]{:S(2)}) collective-permute-start(bf16[256,4096]{1,0:T(8,128)(2,1)S(1)} %collective-permute-done.4), channel_id=1, source_target_pairs={{0,4},{4,8},{8,12},{12,16},{16,20},{20,24},{24,28},{28,0},{1,5},{5... | collective-permute-start | bytes 6291464 | tf_op jit(solution)/shard_map/ppermute | solution.py:46
  300.8 65.2 %collective-permute-start.6 = (bf16[256,4096]{1,0:T(8,128)(2,1)}, bf16[256,4096]{1,0:T(8,128)(2,1)}, u32[]{:S(2)}, u32[]{:S(2)}) collective-permute-start(bf16[256,4096]{1,0:T(8,128)(2,1)} %collective-permute-done.5), channel_id=1, source_target_pairs={{0,4},{4,8},{8,12},{12,16},{16,20},{20,24},{24,28},{28,0},{1,5},{5... | collective-permute-start | bytes 6291464 | tf_op jit(solution)/shard_map/ppermute | solution.py:46
  306.2 79.0 %all-to-all-start = ((bf16[256,8,640]{2,0,1:T(8,128)(2,1)}), bf16[256,8,640]{2,0,1:T(8,128)(2,1)}, u32[]{:S(2)}, u32[]{:S(2)}) async-start(bf16[256,8,640]{2,0,1:T(8,128)(2,1)} %copy.11), calls=%async_computation | async-start | bytes 5242880 | tf_op jit(solution)/shard_map/all_to_all | solution.py:43
  312.2 59.2 %copy-start.7 = (bf16[256,4096]{1,0:T(8,128)(2,1)S(1)}, bf16[256,4096]{1,0:T(8,128)(2,1)}, u32[]{:S(2)}) copy-start(bf16[256,4096]{1,0:T(8,128)(2,1)} %copy-done.6) | copy-start | bytes 6291460
  312.2 59.4 %copy-start.5 = (bf16[256,4096]{1,0:T(8,128)(2,1)S(1)}, bf16[256,4096]{1,0:T(8,128)(2,1)}, u32[]{:S(2)}) copy-start(bf16[256,4096]{1,0:T(8,128)(2,1)} %copy-done.4) | copy-start | bytes 6291460
  312.2 59.6 %copy-start.3 = (bf16[256,4096]{1,0:T(8,128)(2,1)S(1)}, bf16[256,4096]{1,0:T(8,128)(2,1)}, u32[]{:S(2)}) copy-start(bf16[256,4096]{1,0:T(8,128)(2,1)} %copy-done.2) | copy-start | bytes 6291460
  367.8 4.3 copy-start.1
